TPU v7x, 32 devices: a whole 2x2x4 slice. The times are simulated.
32 devices in a mesh: gx: 4 (over y, x), gy: 8 (over z, core).
Axes of the slice: x: 2, y: 2, z: 4, core: 2. Of those that a mesh axis runs over, the one named last changes fastest.
Arguments:
- right_side: float32 [128, 2048], P('gx', 'gy'), may hold values from -200 to 200
- reaction: float32 [128, 2048], P('gx', 'gy'), may hold values from 2 to 4
- kernel: float32 [65, 65], replicated, may hold values from -0.04 to 0.04
Outputs:
- solution: float32 [128, 2048], P('gx', 'gy')
- residual: float32 [128, 2048], P('gx', 'gy')
All inputs are finite; a program needn't handle non-finite values.
Results may differ from a plain program's by a relative error of at most 0.00075.
Values sent between devices are 32-bit elements; how exact they have to be, the bound alone decides.
A program may use at most 64 MiB of HBM per device.

v0:
```python
import jax
import jax.numpy as jnp
from jax import lax
from jax.sharding import PartitionSpec as P

ITERS = 4


small_term = 1e-06


def extended(block, sides, width):
    for axis, dim in sides:
        count = lax.axis_size(axis)
        forward = [(i, i + 1) for i in range(count - 1)]
        backward = [(target, source) for source, target in forward]
        low = lax.ppermute(
            lax.slice_in_dim(block, block.shape[dim] - width, None, axis=dim), axis, forward
        )
        high = lax.ppermute(lax.slice_in_dim(block, 0, width, axis=dim), axis, backward)
        block = jnp.concatenate([low, block, high], axis=dim)
    return block


def solve_small(normal_matrix, target, count):
    factor = jnp.linalg.cholesky(normal_matrix)
    forward = []
    for position in range(count):
        accum = target[position]
        for earlier in range(position):
            accum = accum - factor[position, earlier] * forward[earlier]
        forward.append(accum / factor[position, position])
    backward = [None] * count
    for position in reversed(range(count)):
        accum = forward[position]
        for later in range(position + 1, count):
            accum = accum - factor[later, position] * backward[later]
        backward[position] = accum / factor[position, position]
    return backward


def total_norm(values):
    return jnp.sqrt(lax.psum(jnp.sum(values * values), ("gx", "gy")) + small_term)


def local(right_side, reaction, kernel):
    tile_rows, tile_cols = right_side.shape
    kernel_width = kernel.shape[0]
    radius = kernel_width // 2
    bundle = 5
    span_rows = tile_rows + 2 * radius
    period = 2 * tile_rows + 2 * radius
    highest = lax.Precision.HIGHEST

    def extend(values):
        return extended(values, (("gx", 0), ("gy", 1)), radius)

    def apply_operator(values):
        padded = extend(values)

        def group_step(group, summed):
            first_col = group * bundle
            chosen = lax.dynamic_slice_in_dim(kernel, first_col, bundle, 1)
            columns_rev = jnp.pad(chosen[::-1, :].T, ((0, 0), (0, period - kernel_width)))
            toeplitz = jnp.tile(columns_rev, (1, tile_rows))[:, : tile_rows * (period - 1)]
            toeplitz = toeplitz.reshape(bundle, tile_rows, period - 1)[:, :, :span_rows]
            for member in range(bundle):
                offset = 2 * radius - first_col - member
                shifted = lax.dynamic_slice_in_dim(padded, offset, tile_cols, 1)
                summed = summed + jnp.dot(
                    toeplitz[member], shifted, precision=highest, preferred_element_type=jnp.float32
                )
            return summed

        convolved = lax.fori_loop(
            0, kernel_width // bundle, group_step, jnp.zeros((tile_rows, tile_cols), jnp.float32)
        )
        return reaction * values - convolved

    initial_norm = total_norm(right_side)
    krylov = [right_side / initial_norm]
    upper = jnp.zeros((ITERS + 1, ITERS), jnp.float32)
    for column in range(ITERS):
        candidate = apply_operator(krylov[column])
        basis_now = jnp.stack(krylov)
        first_terms = jnp.einsum("kij,ij->k", basis_now, candidate, precision=highest)
        first_terms = lax.psum(first_terms, ("gx", "gy"))
        candidate = candidate - jnp.einsum("k,kij->ij", first_terms, basis_now, precision=highest)
        upper = upper.at[: column + 1, column].set(first_terms)
        length = total_norm(candidate)
        upper = upper.at[column + 1, column].set(length)
        krylov.append(candidate / length)
    normal_matrix = jnp.dot(upper.T, upper, precision=highest)
    coeffs = solve_small(normal_matrix, initial_norm * upper[0, :], ITERS)
    solution = coeffs[0] * krylov[0]
    for column in range(1, ITERS):
        solution = solution + coeffs[column] * krylov[column]
    residual = right_side - apply_operator(solution)
    return (solution, residual)


def solution(mesh):
    in_specs = (P("gx", "gy"), P("gx", "gy"), P())
    out_specs = (P("gx", "gy"), P("gx", "gy"))
    return jax.shard_map(local, mesh=mesh, in_specs=in_specs, out_specs=out_specs, check_vma=False)
```

profile of v0, /device:TPU:0, one launch (start us, length us, event | category | flops | bytes accessed | tf_op | source)
XLA Modules:
  0.0 612.4 jit_solution(7024932952548193070)
XLA Ops:
  0.6 1.4 multiply_reduce_fusion.4
  2.1 42.2 %psum.63 = f32[]{:T(128)} all-reduce(f32[]{:T(128)} %multiply_reduce_fusion.4), channel_id=1, replica_groups=mesh['gx'=4,'gy'=8] {'gx','gy'}, use_global_device_ids=true, to_apply=%region_1.0 | all-reduce | flops 1 | bytes 8 | tf_op jit(solution)/shard_map/psum | solution.py:43
  45.0 4.2 collective-permute-start
  49.2 1.3 collective-permute-start.1
  53.1 1.9 collective-permute-done.1
  55.1 1.3 collective-permute-start.2
  56.3 1.3 collective-permute-start.3
  59.0 2.2 collective-permute-done.3
  61.3 24.5 %while.98 = (s32[]{:T(128)}, f32[32,256]{1,0:T(8,128)S(1)}, f32[65,65]{1,0:T(8,128)S(1)}, f32[96,320]{1,0:T(8,128)S(1)}, s32[]{:T(128)}, /*index=5*/s32[]{:T(128...) while((s32[]{:T(128)}, f32[32,256]{1,0:T(8,128)S(1)}, ...), condition=%wide.region_3.4_spmd.clone, body=%wide.region_2.3_spmd.clone.sunk | while | flops 47235088 | bytes 1324147 | solution.py:75
  86.5 42.6 %psum.64 = f32[1]{0:T(128)} all-reduce(f32[1]{0:T(128)} %bitcast), channel_id=1, replica_groups=mesh['gx'=4,'gy'=8] {'gx','gy'}, use_global_device_ids=true, to_apply=%region_4.5 | all-reduce | flops 1 | bytes 8 | tf_op jit(solution)/shard_map/psum | solution.py:87
  129.1 1.3 multiply_reduce_fusion.3
  130.5 39.5 %psum.65 = f32[]{:T(128)} all-reduce(f32[]{:T(128)} %get-tuple-element.963), channel_id=1, replica_groups=mesh['gx'=4,'gy'=8] {'gx','gy'}, use_global_device_ids=true, to_apply=%region_6.7 | all-reduce | flops 1 | bytes 8 | tf_op jit(solution)/shard_map/psum | solution.py:43
  170.6 4.2 collective-permute-start.4
  174.8 1.3 collective-permute-start.5
  176.4 4.2 collective-permute-done.5
  182.0 1.3 collective-permute-start.7
  183.3 3.6 collective-permute-done.7
  187.1 24.5 %while.99 = (s32[]{:T(128)}, f32[32,256]{1,0:T(8,128)S(1)}, f32[65,65]{1,0:T(8,128)S(1)}, f32[96,320]{1,0:T(8,128)S(1)}, s32[]{:T(128)}, /*index=5*/s32[]{:T(128...) while((s32[]{:T(128)}, f32[32,256]{1,0:T(8,128)S(1)}, ...), condition=%wide.region_9.10_spmd.clone, body=%wide.region_8.9_spmd.clone.sunk | while | flops 47235088 | bytes 1324147 | solution.py:75
  212.9 42.5 %psum.66 = f32[2]{0:T(128)S(1)} all-reduce(f32[2]{0:T(128)S(1)} %convolution_bitcast_fusion.2), channel_id=1, replica_groups=mesh['gx'=4,'gy'=8] {'gx','gy'}, use_global_device_ids=true, to_apply=%region_10.11 | all-reduce | flops 2 | bytes 16 | tf_op jit(solution)/shard_map/psum | solution.py:87
  256.5 39.1 %psum.67 = f32[]{:T(128)} all-reduce(f32[]{:T(128)} %multiply_reduce_fusion.2), channel_id=1, replica_groups=mesh['gx'=4,'gy'=8] {'gx','gy'}, use_global_device_ids=true, to_apply=%region_12.13 | all-reduce | flops 1 | bytes 8 | tf_op jit(solution)/shard_map/psum | solution.py:43
  296.3 4.2 collective-permute-start.8
  300.5 1.3 collective-permute-start.9
  301.8 1.9 broadcast_select_fusion.2
  303.7 2.6 collective-permute-done.9
  307.7 1.3 collective-permute-start.11
  309.0 3.7 collective-permute-done.11
  312.8 24.5 %while.100 = (s32[]{:T(128)}, f32[32,256]{1,0:T(8,128)S(1)}, f32[65,65]{1,0:T(8,128)S(1)}, f32[96,320]{1,0:T(8,128)S(1)}, s32[]{:T(128)}, /*index=5*/s32[]{:T(12...) while((s32[]{:T(128)}, f32[32,256]{1,0:T(8,128)S(1)}, ...), condition=%wide.region_15.16_spmd.clone, body=%wide.region_14.15_spmd.clone.sunk | while | flops 47235088 | bytes 1324147 | solution.py:75
  337.9 1.4 scatter.30
  339.4 42.4 %psum.68 = f32[3]{0:T(128)S(1)} all-reduce(f32[3]{0:T(128)S(1)} %convolution_bitcast_fusion.1), channel_id=1, replica_groups=mesh['gx'=4,'gy'=8] {'gx','gy'}, use_global_device_ids=true, to_apply=%region_16.17 | all-reduce | flops 3 | bytes 24 | tf_op jit(solution)/shard_map/psum | solution.py:87
  382.9 39.1 %psum.69 = f32[]{:T(128)} all-reduce(f32[]{:T(128)} %multiply_reduce_fusion.1), channel_id=1, replica_groups=mesh['gx'=4,'gy'=8] {'gx','gy'}, use_global_device_ids=true, to_apply=%region_18.19 | all-reduce | flops 1 | bytes 8 | tf_op jit(solution)/shard_map/psum | solution.py:43
  422.7 4.2 collective-permute-start.12
  426.9 1.3 collective-permute-start.13
  428.2 1.8 broadcast_select_fusion.1
  430.0 2.7 collective-permute-done.13
  434.0 1.5 collective-permute-start.15
  435.6 3.5 collective-permute-done.15
  439.2 24.5 %while.101 = (s32[]{:T(128)}, f32[32,256]{1,0:T(8,128)S(1)}, f32[65,65]{1,0:T(8,128)S(1)}, f32[96,320]{1,0:T(8,128)S(1)}, s32[]{:T(128)}, /*index=5*/s32[]{:T(12...) while((s32[]{:T(128)}, f32[32,256]{1,0:T(8,128)S(1)}, ...), condition=%wide.region_21.22_spmd.clone, body=%wide.region_20.21_spmd.clone.sunk | while | flops 47235088 | bytes 1324147 | solution.py:75
  464.3 1.4 scatter.34
  465.7 42.4 %psum.70 = f32[4]{0:T(128)S(1)} all-reduce(f32[4]{0:T(128)S(1)} %convolution_bitcast_fusion), channel_id=1, replica_groups=mesh['gx'=4,'gy'=8] {'gx','gy'}, use_global_device_ids=true, to_apply=%region_22.23 | all-reduce | flops 4 | bytes 32 | tf_op jit(solution)/shard_map/psum | solution.py:87
  509.2 39.1 %psum.71 = f32[]{:T(128)} all-reduce(f32[]{:T(128)} %fusion.60), channel_id=1, replica_groups=mesh['gx'=4,'gy'=8] {'gx','gy'}, use_global_device_ids=true, to_apply=%region_24.25 | all-reduce | flops 1 | bytes 8 | tf_op jit(solution)/shard_map/psum | solution.py:43
  549.0 1.9 broadcast_select_fusion
  550.9 1.4 scatter.36
  570.8 4.2 collective-permute-start.16
  575.0 1.3 collective-permute-start.17
  576.6 4.2 collective-permute-done.17
  582.2 1.3 collective-permute-start.19
  583.5 3.7 collective-permute-done.19
  587.4 24.5 %while.102 = (s32[]{:T(128)}, f32[32,256]{1,0:T(8,128)S(1)}, f32[65,65]{1,0:T(8,128)S(1)}, f32[96,320]{1,0:T(8,128)S(1)}, s32[]{:T(128)}, /*index=5*/s32[]{:T(12...) while((s32[]{:T(128)}, f32[32,256]{1,0:T(8,128)S(1)}, ...), condition=%wide.region_28.29_spmd.clone, body=%wide.region_27.28_spmd.clone.sunk | while | flops 47235088 | bytes 1324147 | solution.py:75
  (874 shorter events, 134.7 us)
Async XLA Ops:
  0.6 44.3 %copy-start.1 = (f32[32,256]{1,0:T(8,128)S(1)}, f32[32,256]{1,0:T(8,128)}, u32[]{:S(2)}) copy-start(f32[32,256]{1,0:T(8,128)} %param.29) | copy-start | bytes 98308
  45.0 8.1 %collective-permute-start = (f32[32,256]{1,0:T(8,128)S(1)}, f32[32,256]{1,0:T(8,128)S(1)}, u32[]{:S(2)}, u32[]{:S(2)}) collective-permute-start(f32[32,256]{1,0:T(8,128)S(1)} %broadcast_divide_fusion.3), channel_id=1, source_target_pairs={{0,8},{8,16},{16,24},{1,9},{9,17},{17,25},{2,10},{10,18},{18,26},{... | collective-permute-start | bytes 98312 | tf_op jit(solution)/shard_map/ppermute | solution.py:17
  49.2 5.8 collective-permute-start.1
  51.1 0.7 copy-start.5
  51.7 0.7 copy-start.4
  55.1 3.9 collective-permute-start.2
  56.3 4.9 collective-permute-start.3
  59.0 2.4 copy-start
  61.3 24.5 %copy-start.2 = (f32[32,256]{1,0:T(8,128)S(1)}, f32[32,256]{1,0:T(8,128)}, u32[]{:S(2)}) copy-start(f32[32,256]{1,0:T(8,128)} %param.30) | copy-start | bytes 98308
  170.6 5.8 collective-permute-start.4
  174.8 5.8 collective-permute-start.5
  180.7 2.6 collective-permute-start.6
  182.0 5.0 collective-permute-start.7
  296.3 7.4 %collective-permute-start.8 = (f32[32,256]{1,0:T(8,128)S(1)}, f32[32,256]{1,0:T(8,128)S(1)}, u32[]{:S(2)}, u32[]{:S(2)}) collective-permute-start(f32[32,256]{1,0:T(8,128)S(1)} %broadcast_divide_fusion.1), channel_id=1, source_target_pairs={{0,8},{8,16},{16,24},{1,9},{9,17},{17,25},{2,10},{10,18},{18,26},{... | collective-permute-start | bytes 98312 | tf_op jit(solution)/shard_map/ppermute | solution.py:17
  300.5 5.8 collective-permute-start.9
  306.4 2.6 collective-permute-start.10
  307.7 5.0 collective-permute-start.11
  422.7 7.3 %collective-permute-start.12 = (f32[32,256]{1,0:T(8,128)S(1)}, f32[32,256]{1,0:T(8,128)S(1)}, u32[]{:S(2)}, u32[]{:S(2)}) collective-permute-start(f32[32,256]{1,0:T(8,128)S(1)} %broadcast_divide_fusion), channel_id=1, source_target_pairs={{0,8},{8,16},{16,24},{1,9},{9,17},{17,25},{2,10},{10,18},{18,26},{... | collective-permute-start | bytes 98312 | tf_op jit(solution)/shard_map/ppermute | solution.py:17
  426.9 5.8 collective-permute-start.13
  432.8 2.8 collective-permute-start.14
  434.0 5.0 collective-permute-start.15
  570.8 41.0 %copy-start.3 = (f32[32,256]{1,0:T(8,128)}, f32[32,256]{1,0:T(8,128)S(1)}, u32[]{:S(2)}) copy-start(f32[32,256]{1,0:T(8,128)S(1)} %multiply_add_fusion) | copy-start | bytes 98308
  570.8 5.8 collective-permute-start.16
  575.0 5.8 collective-permute-start.17
  580.9 2.6 collective-permute-start.18
  582.2 5.0 collective-permute-start.19
where the time goes:
time: 618 us; the launch traced here: 612 us
  blocking collectives  369 us (60%)
  matrix products  87.7 us (14%)
  starting transfers between devices  40.4 us (7%)
  local copies, waits for them, and re-layouts  37.8 us (6%)
  waiting for transfers between devices  32.8 us (5%)
  between operations  19.8 us (3%)
  other arithmetic  16.1 us (3%)
  loops' own time  8.91 us (1%)
    psum x5, blocking collectives, total_norm(): lax.psum(jnp.sum(values * values), ('gx', 'gy')) + small_term  199 us
    psum x4, blocking collectives, local(): first_terms = lax.psum(first_terms, ('gx', 'gy'))  170 us
    dot_general x325, matrix products, group_step(): jnp.dot(toeplitz[member], shifted, precision=highest, preferred_element_t...  84.5 us
    ppermute x10, waiting for transfers between devices, extended(): lax.ppermute(lax.slice_in_dim(block, 0, width, axis=dim), axis, backward)  32.3 us
    ppermute x10, starting transfers between devices, extended(): lax.ppermute(lax.slice_in_dim(block, block.shape[dim] - width, None, axis...  27.3 us
    ppermute x10, starting transfers between devices, extended(): lax.ppermute(lax.slice_in_dim(block, 0, width, axis=dim), axis, backward)  13.1 us
    reshape x65, local copies, waits for them, and re-layouts, group_step(): toeplitz = toeplitz.reshape(bundle, tile_rows, period - 1)[:, :, :span_rows]  12.6 us
  transfers between devices with their start and end apart: 20, of which 12 were waited for; matrix products, arithmetic and copies ran while one was open for 1% of the time, Pallas kernels for 0%

commit v1 on v0

v1 whole, which is shorter than its diff:
```python
import functools

import jax
import jax.numpy as jnp
from jax import lax
from jax.experimental import pallas as pl
from jax.experimental.pallas import tpu as pltpu
from jax.sharding import PartitionSpec as P

ITERS = 4
SHIFT = 3.0
SMALL = 1e-06
LANES = 128
FOLD = 8
MESH = pl.DeviceIdType.MESH
F32 = jnp.float32
BF16 = jnp.bfloat16


def split(values):
    high = values.astype(BF16)
    return high, (values - high.astype(F32)).astype(BF16)


def lane_group(shape, width):
    return lax.broadcasted_iota(jnp.int32, shape, 1) // width


def pick(group, parts):
    chosen = parts[0]
    for index in range(1, len(parts)):
        chosen = jnp.where(group == index, parts[index], chosen)
    return chosen


def solve(gram):
    count = ITERS + 1
    initial = jnp.sqrt(gram[0][0] + SMALL)
    basis = [[1.0 / initial]]
    images = []
    applied = []
    upper = [[None] * ITERS for _ in range(count)]

    def times_gram(vector):
        out = []
        for row in range(count):
            total = vector[0] * gram[row][0]
            for col in range(1, len(vector)):
                total = total + vector[col] * gram[row][col]
            out.append(total)
        return out

    def inner(left, right):
        total = left[0] * right[0]
        for index in range(1, len(left)):
            total = total + left[index] * right[index]
        return total

    images.append(times_gram(basis[0]))
    for column in range(ITERS):
        prior = basis[column]
        candidate = [SHIFT * prior[0]]
        for index in range(1, len(prior)):
            candidate.append(SHIFT * prior[index] + prior[index - 1])
        candidate.append(prior[-1])
        applied.append(list(candidate))
        for earlier in range(column + 1):
            projected = inner(candidate, images[earlier])
            for index, value in enumerate(basis[earlier]):
                candidate[index] = candidate[index] - projected * value
            upper[earlier][column] = projected
        square = jnp.maximum(inner(candidate, times_gram(candidate)), 0.0)
        length = jnp.sqrt(square + SMALL)
        upper[column + 1][column] = length
        if column + 1 < ITERS:
            inverse = 1.0 / length
            basis.append([value * inverse for value in candidate])
            images.append(times_gram(basis[-1]))

    normal = [[None] * ITERS for _ in range(ITERS)]
    for row in range(ITERS):
        for col in range(row + 1):
            total = None
            for index in range(col + 2):
                term = upper[index][row] * upper[index][col]
                total = term if total is None else total + term
            normal[row][col] = total
    factor = [[None] * ITERS for _ in range(ITERS)]
    inverse = [None] * ITERS
    for col in range(ITERS):
        for row in range(col, ITERS):
            accum = normal[row][col]
            for index in range(col):
                accum = accum - factor[row][index] * factor[col][index]
            if row == col:
                factor[row][col] = jnp.sqrt(accum)
                inverse[col] = 1.0 / factor[row][col]
            else:
                factor[row][col] = accum * inverse[col]
    forward = []
    for row in range(ITERS):
        accum = initial * upper[0][row]
        for index in range(row):
            accum = accum - factor[row][index] * forward[index]
        forward.append(accum * inverse[row])
    coeffs = [None] * ITERS
    for row in reversed(range(ITERS)):
        accum = forward[row]
        for index in range(row + 1, ITERS):
            accum = accum - factor[index][row] * coeffs[index]
        coeffs[row] = accum * inverse[row]

    def combine(vectors, size):
        out = []
        for index in range(size):
            total = None
            for coeff, vector in zip(coeffs, vectors):
                if index < len(vector):
                    term = coeff * vector[index]
                    total = term if total is None else total + term
            out.append(total)
        return out

    return combine(basis, ITERS), combine(applied, count)


def kernel(
    nx, ny, b_ref, reac_ref, k_ref, x_ref, r_ref,
    kpad, whi, wlo, ybuf, wbuf, ebuf, hrow, hedge, gall, gown,
    row_send, row_recv, edge_send, edge_recv, g_send, g_recv,
):
    rows, cols = b_ref.shape
    width = k_ref.shape[0]
    rad = width // 2
    span = rows + 2 * rad
    tiles = cols // LANES
    subs = rows // 8
    count = nx * ny
    gx, gy = lax.axis_index("gx"), lax.axis_index("gy")
    me = gx * ny + gy

    hrow[...] = jnp.zeros_like(hrow)
    hedge[...] = jnp.zeros_like(hedge)

    barrier = pltpu.get_barrier_semaphore()

    def other(step):
        target = lax.rem(me + step, count)
        return (target // ny, lax.rem(target, ny))

    def greet(step, carry):
        pl.semaphore_signal(barrier, inc=1, device_id=other(step), device_id_type=MESH)
        return carry

    lax.fori_loop(1, count, greet, 0)

    exists_x = {-1: gx > 0, 0: None, 1: gx < nx - 1}
    exists_y = {-1: gy > 0, 1: gy < ny - 1}

    def both(dx, dy):
        if dx == 0:
            return exists_y[dy]
        if dy == 0:
            return exists_x[dx]
        return jnp.logical_and(exists_x[dx], exists_y[dy])

    def source(step):
        return b_ref if step == 0 else wbuf.at[step - 1]

    def row_copy(step, dx):
        slot = 0 if dx == 1 else 1
        return pltpu.make_async_remote_copy(
            src_ref=source(step), dst_ref=hrow.at[step, slot],
            send_sem=row_send.at[step, slot], recv_sem=row_recv.at[step, slot],
            device_id=(gx + dx, gy), device_id_type=MESH,
        )

    def edge_copy(step, dx, dy):
        side = 1 if dy == -1 else 0
        group = 1 - dx
        return pltpu.make_async_remote_copy(
            src_ref=ebuf.at[step, side], dst_ref=hedge.at[step, side, group],
            send_sem=edge_send.at[step, side, group], recv_sem=edge_recv.at[step, side, group],
            device_id=(gx + dx, gy + dy), device_id_type=MESH,
        )

    edges = [(dx, dy) for dx in (-1, 1, 0) for dy in (-1, 1)]

    def start_all(step):
        for dx in (-1, 1):
            pl.when(both(dx, 0))(lambda dx=dx: row_copy(step, dx).start())
        for dx, dy in edges:
            pl.when(both(dx, dy))(lambda dx=dx, dy=dy: edge_copy(step, dx, dy).start())

    def wait_recv_all(step):
        for dx in (-1, 1):
            pl.when(both(-dx, 0))(lambda dx=dx: row_copy(step, dx).wait_recv())
        for dx, dy in edges:
            pl.when(both(-dx, -dy))(lambda dx=dx, dy=dy: edge_copy(step, dx, dy).wait_recv())

    def wait_send_all(step):
        for dx in (-1, 1):
            pl.when(both(dx, 0))(lambda dx=dx: row_copy(step, dx).wait_send())
        for dx, dy in edges:
            pl.when(both(dx, dy))(lambda dx=dx, dy=dy: edge_copy(step, dx, dy).wait_send())

    group8 = lane_group((8, LANES), rad)

    def pack_edges(step, values):
        first = values[:, :LANES]
        last = values[:, cols - LANES:]
        lefts, rights = [], []
        for t in range(subs):
            piece = first[8 * t: 8 * t + 8]
            lefts.append(pltpu.roll(piece, (rad * t) % LANES, 1) if t else piece)
            piece = last[8 * t: 8 * t + 8]
            move = (rad * t - (LANES - rad)) % LANES
            rights.append(pltpu.roll(piece, move, 1) if move else piece)
        ebuf[step, 1] = pick(group8, lefts)
        ebuf[step, 0] = pick(group8, rights)

    pack_edges(0, b_ref[...])

    kpad[...] = jnp.zeros_like(kpad)
    kpad[:width, :width] = k_ref[...]
    kpad[...] = kpad[...].T
    group_span = lane_group((span, LANES), rows)
    per_tile = LANES // rows
    blocks = -(-width // (2 * FOLD))
    whole = FOLD * rows
    for q in range(blocks):
        for h in range(2):
            first = 2 * FOLD * q + FOLD * h
            base = (2 * q + h) * LANES
            for t in range(whole // LANES):
                parts = []
                for u in range(per_tile):
                    b = first + per_tile * t + u
                    if b < width:
                        line = jnp.broadcast_to(kpad[b: b + 1, :], (span, LANES))
                        move = (rows * u - 2 * rad) % LANES
                        parts.append(pltpu.roll(line, move, 1, stride=1, stride_axis=0))
                    else:
                        parts.append(jnp.zeros((span, LANES), F32))
                block = pick(group_span, parts)
                block = jnp.concatenate([block, jnp.zeros((LANES - span, LANES), F32)], axis=0)
                high, low = split(block)
                whi[base: base + LANES, t * LANES: (t + 1) * LANES] = high
                wlo[base: base + LANES, t * LANES: (t + 1) * LANES] = low

    pl.semaphore_wait(barrier, count - 1)
    start_all(0)

    steps_m = cols + 2 * FOLD
    group_cols = lane_group((cols, LANES), rows)
    offset = reac_ref[...] - SHIFT

    def fold8(values):
        total = values[:8]
        for t in range(1, subs):
            total = total + values[8 * t: 8 * t + 8]
        out = total[:, :LANES]
        for t in range(1, tiles):
            out = out + total[:, t * LANES: (t + 1) * LANES]
        return jnp.sum(out, axis=0, keepdims=True)

    vectors = [b_ref[...]]
    products = {(0, 0): fold8(vectors[0] * vectors[0])}

    for step in range(ITERS):
        own = vectors[step]
        wait_recv_all(step)
        above, below = hrow[step, 0], hrow[step, 1]
        blank = jnp.zeros((LANES - span, LANES), F32)
        centre = []
        for t in range(tiles):
            part = slice(t * LANES, (t + 1) * LANES)
            tile = jnp.concatenate([above[:, part], own[:, part], below[:, part], blank], axis=0)
            centre.append(tile.T)
        sides = []
        for group in range(3):
            left = hedge[step, 0, group]
            right = hedge[step, 1, group] if True else None
            for t in range(subs):
                move = (-rad * t) % LANES
                from_left = pltpu.roll(left, move, 1) if move else left
                move = (rad - rad * t) % LANES
                from_right = pltpu.roll(right, move, 1) if move else right
                sides.append(jnp.where(group8 == 0, from_left, from_right))
        side = jnp.concatenate(sides + [blank], axis=0).T
        padded = jnp.concatenate([side[:rad]] + centre + [side[rad: 2 * rad]], axis=0)
        zero = jnp.zeros((FOLD, LANES), F32)
        plain = jnp.concatenate([zero] * 3 + [padded] + [zero], axis=0)
        moved = jnp.concatenate([zero] * 4 + [padded], axis=0)
        high, low = split(jnp.concatenate([plain, moved], axis=1))
        top = 2 * FOLD * blocks
        take = lambda m: jnp.concatenate(
            [m[top - 2 * FOLD * q: top - 2 * FOLD * q + steps_m] for q in range(blocks)], axis=1
        )
        lhs_high, lhs_low = take(high), take(low)
        dot = functools.partial(jnp.dot, preferred_element_type=F32)
        ybuf[...] = dot(lhs_high, whi[...]) + dot(lhs_low, whi[...]) + dot(lhs_high, wlo[...])
        parts = []
        for u in range(per_tile):
            total = None
            for t in range(whole // LANES):
                start = FOLD - per_tile * t - u
                piece = ybuf[start: start + cols, t * LANES: (t + 1) * LANES]
                total = piece if total is None else total + piece
            parts.append(total)
        chosen = pick(group_cols, parts)
        pieces = []
        for t in range(tiles):
            turned = chosen[t * LANES: (t + 1) * LANES].T
            total = turned[:rows]
            for u in range(1, per_tile):
                total = total + turned[rows * u: rows * (u + 1)]
            pieces.append(total)
        fresh = offset * own - jnp.concatenate(pieces, axis=1)
        wbuf[step] = fresh
        if step + 1 < ITERS:
            pack_edges(step + 1, fresh)
            start_all(step + 1)
        vectors.append(fresh)
        for earlier in range(step + 2):
            products[(earlier, step + 1)] = fold8(vectors[earlier] * fresh)

    order = sorted(products)
    stack = [products[pair] for pair in order]
    table = jnp.concatenate(stack + [jnp.zeros((LANES - len(stack), LANES), F32)], axis=0)
    line = jnp.sum(table.T, axis=0, keepdims=True)
    gown[...] = line
    gall[me] = line

    def gram_copy(step):
        return pltpu.make_async_remote_copy(
            src_ref=gown, dst_ref=gall.at[me],
            send_sem=g_send.at[step], recv_sem=g_recv.at[me],
            device_id=other(step), device_id_type=MESH,
        )

    def gram_arrival(step):
        sender = lax.rem(me + step, count)
        return pltpu.make_async_remote_copy(
            src_ref=gown, dst_ref=gall.at[sender],
            send_sem=g_send.at[step], recv_sem=g_recv.at[sender],
            device_id=other(step), device_id_type=MESH,
        )

    def send(step, carry):
        gram_copy(step).start()
        return carry

    def receive(step, carry):
        gram_arrival(step).wait_recv()
        return carry

    def sent(step, carry):
        gram_copy(step).wait_send()
        return carry

    lax.fori_loop(1, count, send, 0)
    for step in range(ITERS):
        wait_send_all(step)
    lax.fori_loop(1, count, receive, 0)
    total = jnp.sum(gall[...], axis=0)
    spread = jnp.broadcast_to(total, (LANES, LANES)).T
    gram = [[None] * (ITERS + 1) for _ in range(ITERS + 1)]
    for index, (i, j) in enumerate(order):
        gram[i][j] = gram[j][i] = spread[index: index + 1]
    at_solution, at_applied = solve(gram)
    wide = lambda value: jnp.concatenate([value] * tiles, axis=1)
    answer = wide(at_solution[0]) * vectors[0]
    for index in range(1, ITERS):
        answer = answer + wide(at_solution[index]) * vectors[index]
    x_ref[...] = answer
    image = wide(at_applied[0]) * vectors[0]
    for index in range(1, ITERS + 1):
        image = image + wide(at_applied[index]) * vectors[index]
    r_ref[...] = vectors[0] - image
    lax.fori_loop(1, count, sent, 0)


def solution(mesh):
    nx, ny = mesh.shape["gx"], mesh.shape["gy"]
    count = nx * ny

    def local(right_side, reaction, weights):
        rows, cols = right_side.shape
        width = weights.shape[0]
        blocks = -(-width // (2 * FOLD))
        depth = blocks * 2 * LANES
        block = jax.ShapeDtypeStruct((rows, cols), F32)
        in_vmem = pl.BlockSpec(memory_space=pltpu.VMEM)
        dma = pltpu.SemaphoreType.DMA
        return pl.pallas_call(
            functools.partial(kernel, nx, ny),
            name="gmres_cycle",
            out_shape=(block, block),
            in_specs=[in_vmem] * 3,
            out_specs=(in_vmem, in_vmem),
            scratch_shapes=[
                pltpu.VMEM((LANES, LANES), F32),
                pltpu.VMEM((depth, FOLD * rows), BF16),
                pltpu.VMEM((depth, FOLD * rows), BF16),
                pltpu.VMEM((cols + 2 * FOLD, FOLD * rows), F32),
                pltpu.VMEM((ITERS, rows, cols), F32),
                pltpu.VMEM((ITERS, 2, 8, LANES), F32),
                pltpu.VMEM((ITERS, 2, rows, cols), F32),
                pltpu.VMEM((ITERS, 2, 3, 8, LANES), F32),
                pltpu.VMEM((count, 1, LANES), F32),
                pltpu.VMEM((1, LANES), F32),
                dma((ITERS, 2)), dma((ITERS, 2)),
                dma((ITERS, 2, 3)), dma((ITERS, 2, 3)),
                dma((count,)), dma((count,)),
            ],
            compiler_params=pltpu.CompilerParams(collective_id=0, has_side_effects=True),
        )(right_side, reaction, weights)

    return jax.shard_map(
        local, mesh=mesh,
        in_specs=(P("gx", "gy"), P("gx", "gy"), P()),
        out_specs=(P("gx", "gy"), P("gx", "gy")),
        check_vma=False,
    )
```

time: 618 us -> 37.9 us (0.06)
  blocking collectives: 369 us -> 0 us
  matrix products: 87.7 us -> 0 us
  starting transfers between devices: 40.4 us -> 0 us
  local copies, waits for them, and re-layouts: 37.8 us -> 2 us
  Pallas kernels: 0 us -> 35 us
  waiting for transfers between devices: 32.8 us -> 0 us
  between operations: 19.8 us -> 0.65 us
  other arithmetic: 16.1 us -> 0 us
  loops' own time: 8.91 us -> 0 us
    psum x9 -> x0, blocking collectives: 369 us -> none  [the longest x5 199 us: total_norm(): lax.psum(jnp.sum(values * values), ('gx', 'gy')) + small_term]
    dot_general x332 -> x0, matrix products: 87.7 us -> none  [the longest x325 84.5 us: group_step(): jnp.dot(toeplitz[member], shifted, precision=highest, preferred_element_t...]
    ppermute x20 -> x0, starting transfers between devices: 40.4 us -> none  [the longest x10 27.3 us: extended(): lax.ppermute(lax.slice_in_dim(block, block.shape[dim] - width, None, axis...]
    pallas_call x0 -> x1, Pallas kernels: none -> 35 us  [local(): pl.pallas_call(functools.partial(kernel, nx, ny), name='gmres_cycle', out...]
    ppermute x20 -> x0, waiting for transfers between devices: 32.8 us -> none  [the longest x10 32.3 us: extended(): lax.ppermute(lax.slice_in_dim(block, 0, width, axis=dim), axis, backward)]
    reshape x65 -> x0, local copies, waits for them, and re-layouts: 12.6 us -> none  [group_step(): toeplitz = toeplitz.reshape(bundle, tile_rows, period - 1)[:, :, :span_rows]]
    while x195 -> x0, local copies, waits for them, and re-layouts: 9.34 us -> none
    another operation x5 -> x0, loops' own time: 8.91 us -> none  [apply_operator(): lax.fori_loop(0, kernel_width // bundle, group_step, jnp.zeros((tile_rows...]
  transfers between devices with their start and end apart: 20 -> 0, of which waited for: 12 -> 0; matrix products, arithmetic and copies ran while one was open for 1% -> 0% of each run, Pallas kernels for 0% -> 0%
where the time goes in v1:
time: 37.9 us; the launch traced here: 37.6 us
  Pallas kernels  35 us (92%)
  local copies, waits for them, and re-layouts  2 us (5%)
  between operations  0.65 us (2%)
    pallas_call x1, Pallas kernels, local(): pl.pallas_call(functools.partial(kernel, nx, ny), name='gmres_cycle', out...  35 us
    unnamed x4, local copies, waits for them, and re-layouts  2 us

profile of v1, /device:TPU:0, one launch (start us, length us, event | category | flops | bytes accessed | tf_op | source)
XLA Modules:
  0.0 37.6 jit_solution(10701521722283879571)
XLA Ops:
  0.6 35.0 %gmres_cycle.1 = (f32[32,256]{1,0:T(8,128)}, f32[32,256]{1,0:T(8,128)}) custom-call(f32[32,256]{1,0:T(8,128)} %b_ref.1, f32[32,256]{1,0:T(8,128)} %reac_ref.1, f32[65,65]{1,0:T(8,128)} %k_ref.1), custom_call_target="tpu_custom_call" | custom-call | tf_op jit(solution)/shard_map/gmres_cycle/pallas_call | solution.py:396
  35.6 0.0 copy-start
  35.6 1.4 %copy.7 = f32[32,256]{1,0:T(8,128)} copy(f32[32,256]{1,0:T(8,128)} %get-tuple-element.4) | data formatting | bytes 65536
  37.0 0.0 copy-done
  37.0 0.6 %copy.8 = f32[32,256]{1,0:T(8,128)} copy(f32[32,256]{1,0:T(8,128)S(1)} %copy-done) | data formatting | bytes 65536
Async XLA Ops:
  35.6 1.4 %copy-start = (f32[32,256]{1,0:T(8,128)S(1)}, f32[32,256]{1,0:T(8,128)}, u32[]{:S(2)}) copy-start(f32[32,256]{1,0:T(8,128)} %get-tuple-element.5) | copy-start | bytes 98308

commit v2 on v1

--- a/solution.py
+++ b/solution.py
@@ -264,6 +264,34 @@
             out = out + total[:, t * LANES: (t + 1) * LANES]
         return jnp.sum(out, axis=0, keepdims=True)
 
+    def multiply(lhs_tiles, *accs):
+        work = [(whi, q, lhs_tiles[q]) for q in range(blocks)] + [(wlo, q, lhs_tiles[q][:1]) for q in range(blocks)]
+        lanes_of = [[], []]
+        load = [0, 0]
+        for item in work:
+            unit = 0 if load[0] <= load[1] else 1
+            lanes_of[unit].append(item)
+            load[unit] += len(item[2])
+        def push(unit, index):
+            table, q, _ = lanes_of[unit][index]
+            pltpu.matmul_push_rhs(
+                table[q * 2 * LANES: (q + 1) * 2 * LANES, :], staging_register=index % 2, mxu_index=unit
+            )
+        for unit in range(2):
+            push(unit, 0)
+        for index in range(max(map(len, lanes_of))):
+            for unit in range(2):
+                if index + 1 < len(lanes_of[unit]):
+                    push(unit, index + 1)
+            for unit in range(2):
+                if index < len(lanes_of[unit]):
+                    for place, lhs in enumerate(lanes_of[unit][index][2]):
+                        pltpu.matmul_acc_lhs(
+                            accs[unit], lhs, load_staged_rhs=index % 2 if place == 0 else None
+                        )
+        parts = [pltpu.matmul_pop(accs[unit]) for unit in range(2)]
+        ybuf[...] = parts[0] + parts[1]
+
     vectors = [b_ref[...]]
     products = {(0, 0): fold8(vectors[0] * vectors[0])}
 
@@ -294,12 +322,11 @@
         moved = jnp.concatenate([zero] * 4 + [padded], axis=0)
         high, low = split(jnp.concatenate([plain, moved], axis=1))
         top = 2 * FOLD * blocks
-        take = lambda m: jnp.concatenate(
-            [m[top - 2 * FOLD * q: top - 2 * FOLD * q + steps_m] for q in range(blocks)], axis=1
-        )
-        lhs_high, lhs_low = take(high), take(low)
-        dot = functools.partial(jnp.dot, preferred_element_type=F32)
-        ybuf[...] = dot(lhs_high, whi[...]) + dot(lhs_low, whi[...]) + dot(lhs_high, wlo[...])
+        lhs_tiles = [
+            (high[top - 2 * FOLD * q: top - 2 * FOLD * q + steps_m], low[top - 2 * FOLD * q: top - 2 * FOLD * q + steps_m])
+            for q in range(blocks)
+        ]
+        pl.run_scoped(functools.partial(multiply, lhs_tiles), *[pltpu.ACC(unit)(ybuf.shape, F32) for unit in range(2)])
         parts = []
         for u in range(per_tile):
             total = None

time: 37.9 us -> 35.9 us (0.947)
  Pallas kernels: 35 us -> 33 us
    pallas_call x1, Pallas kernels: 35 us -> 33 us  [local(): pl.pallas_call(functools.partial(kernel, nx, ny), name='gmres_cycle', out...]
where the time goes in v2:
time: 35.9 us; the launch traced here: 35.7 us
  Pallas kernels  33 us (92%)
  local copies, waits for them, and re-layouts  2 us (6%)
  between operations  0.65 us (2%)
    pallas_call x1, Pallas kernels, local(): pl.pallas_call(functools.partial(kernel, nx, ny), name='gmres_cycle', out...  33 us
    unnamed x4, local copies, waits for them, and re-layouts  2 us

profile of v2, /device:TPU:0, one launch (start us, length us, event | category | flops | bytes accessed | tf_op | source)
XLA Modules:
  0.0 35.7 jit_solution(9270123746725062505)
XLA Ops:
  0.6 33.0 %gmres_cycle.1 = (f32[32,256]{1,0:T(8,128)}, f32[32,256]{1,0:T(8,128)}) custom-call(f32[32,256]{1,0:T(8,128)} %b_ref.1, f32[32,256]{1,0:T(8,128)} %reac_ref.1, f32[65,65]{1,0:T(8,128)} %k_ref.1), custom_call_target="tpu_custom_call" | custom-call | tf_op jit(solution)/shard_map/gmres_cycle/pallas_call | solution.py:423
  33.7 0.0 copy-start
  33.7 1.4 %copy.7 = f32[32,256]{1,0:T(8,128)} copy(f32[32,256]{1,0:T(8,128)} %get-tuple-element.4) | data formatting | bytes 65536
  35.1 0.0 copy-done
  35.1 0.6 %copy.8 = f32[32,256]{1,0:T(8,128)} copy(f32[32,256]{1,0:T(8,128)S(1)} %copy-done) | data formatting | bytes 65536
Async XLA Ops:
  33.7 1.4 %copy-start = (f32[32,256]{1,0:T(8,128)S(1)}, f32[32,256]{1,0:T(8,128)}, u32[]{:S(2)}) copy-start(f32[32,256]{1,0:T(8,128)} %get-tuple-element.5) | copy-start | bytes 98308
